TPU v7x, 512 devices: a whole 4x8x8 slice. The times are simulated.
512 devices in a mesh: cuts: 32 (over z, y_lo), slab: 16 (over x, y_hi, core).
Axes of the slice: x: 4, y: 8 (y_hi: 2, y_lo: 4; y = y_hi * 4 + y_lo), z: 8, core: 2. Of those that a mesh axis runs over, the one named last changes fastest.
Arguments:
- quasi: bfloat16 [2, 192, 16, 9216], P(None, 'cuts', 'slab'), may hold values from -6 to 6
- counts: int32 [32], replicated, may hold values from 1 to 6, 64 in all
- slot_slice: int32 [192], replicated, may hold values from 0 to 15
- occupation: float32 [192], replicated, may hold values from 0.0078125 to 0.0625
- filter_coef: float32 [16, 9], replicated, may hold values from -2.5 to 2.5
- trap_index: int32 [16, 9216], P('slab'), may hold values from 0 to 31
- trap_table: float32 [32], replicated, may hold values from 0 to 1.5
- mean_field: float32 [16, 9216], P('slab'), may hold values from -1.5 to 0
- pairing: float32 [16, 9216], P('slab'), may hold values from 0.2 to 1
Outputs:
- normal_density: float32 [16, 9216], P('slab', 'cuts')
- anomalous_density: float32 [16, 9216], P('slab', 'cuts')
- new_mean_field: float32 [16, 9216], P('slab', 'cuts')
- new_pairing: float32 [16, 9216], P('slab', 'cuts')
Inputs may be any that keep to these rules, and one draw needn't show every extreme that they name: The live vectors of cut c fill the first counts[c] of its 6 slots; the counts sum to 64 and the largest is exactly 6.
All inputs are finite; a program needn't handle non-finite values.
Results may differ from a plain program's by a relative error of at most 0.0003.
Values may be sent and summed in bfloat16 or wider, within the bound.
No kernel may reach another device: no remote copies, remote signals or barrier semaphores. Data moves between devices by JAX's collectives and lax.ppermute only.
A program may use at most 64 MiB of HBM per device.

v0:
```python
import jax
import jax.numpy as jnp
from jax import lax
from jax.sharding import PartitionSpec as P

NX = 96
VEC_DEV = 2
DEGREE = 8
spectral_scale = 8.5
beta_coef = 0.6
chem_level = 1.0
coupling = 1.0
density_floor = 0.05


def shifted(shard, axis, by):
    devices = lax.axis_size(axis)
    pairs = [(i, i + by) for i in range(devices) if 0 <= i + by < devices]
    return lax.ppermute(shard, axis, pairs)


def combine(field, z_lower, z_upper, y_before, y_after, potential, pairing):
    column = jnp.arange(field.shape[-1]) % NX
    left_ok = (column > 0).astype(jnp.float32)
    right_ok = (column < NX - 1).astype(jnp.float32)
    x_before = jnp.concatenate([jnp.zeros_like(field[..., :1]), field[..., :-1]], axis=3)
    x_after = jnp.concatenate([field[..., 1:], jnp.zeros_like(field[..., :1])], axis=3)
    beside_all = z_lower + z_upper + y_before + y_after
    beside_all = beside_all + x_after * right_ok + x_before * left_ok
    single = 0.5 * (6.0 * field - beside_all) + potential * field
    upper = single[0] + pairing * field[1]
    lower = pairing * field[0] - single[1]
    return jnp.stack([upper, lower]) / spectral_scale


def plane_edges(field):
    below = shifted(field, "slab", 1)
    above = shifted(field, "slab", -1)
    z_lower = jnp.concatenate([below, field[:, :, :-1]], axis=2)
    z_upper = jnp.concatenate([field[:, :, 1:], above], axis=2)
    return (z_lower, z_upper)


def remote_rows(field):
    before = shifted(field[..., -NX:], "cuts", 1)
    after = shifted(field[..., :NX], "cuts", -1)
    y_before = jnp.concatenate([before, field[..., :-NX]], axis=3)
    y_after = jnp.concatenate([field[..., NX:], after], axis=3)
    return (y_before, y_after)


def apply_block(field, potential, pairing, row_source):
    z_lower, z_upper = plane_edges(field)
    y_before, y_after = row_source(field)
    return combine(field, z_lower, z_upper, y_before, y_after, potential, pairing)


def chebyshev(vectors, coefs, operator):
    previous = vectors
    current = operator(vectors)
    filtered = (
        coefs[:, 0][None, :, None, None] * previous + coefs[:, 1][None, :, None, None] * current
    )
    for order in range(2, DEGREE + 1):
        following = 2.0 * operator(current) - previous
        filtered = filtered + coefs[:, order][None, :, None, None] * following
        previous, current = (current, following)
    return filtered


def trap_lookup(index_block, trap_table):
    levels = jnp.arange(trap_table.shape[0])
    onehot = (index_block[:, None, :] == levels[None, :, None]).astype(jnp.float32)
    return jnp.einsum("l,zlf->zf", trap_table, onehot, precision=lax.Precision.HIGHEST)


def slice_coefs(slot_ids, filter_coef):
    levels = jnp.arange(filter_coef.shape[0])
    onehot = (slot_ids[:, None] == levels[None, :]).astype(jnp.float32)
    return jnp.dot(onehot, filter_coef, precision=lax.Precision.HIGHEST)


def body(
    quasi, counts, slot_slice, occupation, filter_coef, trap_index, trap_table, mean_field, pairing
):
    cut_count = lax.axis_size("cuts")
    device = lax.axis_index("cuts")
    cap = quasi.shape[1]
    flat = quasi.shape[3]
    share = flat // cut_count
    offset = device * share
    mean_local = lax.dynamic_slice_in_dim(mean_field, offset, share, 1)
    pairing_local = lax.dynamic_slice_in_dim(pairing, offset, share, 1)
    index_local = lax.dynamic_slice_in_dim(trap_index, offset, share, 1)
    potential = trap_lookup(index_local, trap_table) + mean_local
    moved = lax.all_to_all(quasi, "cuts", split_axis=3, concat_axis=1, tiled=True)
    total_live = VEC_DEV * cut_count
    ends = jnp.cumsum(counts)
    starts = ends - counts
    global_ids = jnp.arange(total_live)
    owner = jnp.sum((ends[None, :] <= global_ids[:, None]).astype(jnp.int32), axis=1)
    owners = jnp.arange(cut_count)
    first = jnp.sum(jnp.where(owners[None, :] == owner[:, None], starts[None, :], 0), axis=1)
    row_ids = owner * cap + global_ids - first
    gathered = jnp.take(moved, row_ids, axis=1).astype(jnp.float32)
    weights = jnp.take(occupation, row_ids)
    coefs = slice_coefs(jnp.take(slot_slice, row_ids), filter_coef)

    def operator(field):
        return apply_block(field, potential, pairing_local, remote_rows)

    filtered = chebyshev(gathered, coefs, operator)
    normal = jnp.sum(weights[:, None, None] * filtered[1] * filtered[1], axis=0)
    anomal = jnp.sum(weights[:, None, None] * filtered[0] * filtered[1], axis=0)
    sums = jnp.stack([normal, anomal])
    normal_density = sums[0]
    anomalous_density = sums[1]
    cube_root = jnp.cbrt(normal_density + density_floor)
    new_mean_field = 0.5 * mean_local + 0.5 * (beta_coef * cube_root * cube_root - chem_level)
    new_pairing = 0.5 * pairing_local - coupling * anomalous_density
    return (normal_density, anomalous_density, new_mean_field, new_pairing)


def solution(mesh):
    return jax.shard_map(
        body,
        mesh=mesh,
        in_specs=(
            P(None, "cuts", "slab", None),
            P(),
            P(),
            P(),
            P(),
            P("slab", None),
            P(),
            P("slab", None),
            P("slab", None),
        ),
        out_specs=(P("slab", "cuts"), P("slab", "cuts"), P("slab", "cuts"), P("slab", "cuts")),
        check_vma=False,
    )
```

profile of v0, /device:TPU:262, one launch (start us, length us, event | category | flops | bytes accessed | tf_op | source)
XLA Modules:
  0.0 266.4 jit_solution(4430877389182085189)
XLA Ops:
  0.7 9.5 %copy.32 = bf16[2,6,1,9216]{1,0,2,3:T(2,128)(2,1)} copy(bf16[2,6,1,9216]{3,0,2,1:T(2,128)(2,1)} %param.9) | data formatting | bytes 442368 | tf_op args[0]
  10.2 11.4 %reshape.1740 = bf16[32,2,1728]{2,1,0:T(2,128)(2,1)} reshape(bf16[9216,1,2,6]{3,2,1,0:T(2,128)(2,1)} %bitcast.79) | data formatting | bytes 442368
  21.6 10.4 %all-to-all-start = ((bf16[32,2,1728]{2,1,0:T(2,128)(2,1)}), bf16[32,2,1728]{2,1,0:T(2,128)(2,1)S(1)}, u32[]{:S(2)}, u32[]{:S(2)}) async-start(bf16[32,2,1728]{2,1,0:T(2,128)(2,1)} %reshape.1740), calls=%async_computation | async-start | bytes 458752 | tf_op jit(solution)/shard_map/all_to_all | solution.py:96
  32.5 0.8 gather_fusion
  33.5 0.8 fusion.67
  34.2 0.8 gather_fusion.1
  35.2 0.9 fusion
  36.1 3.4 %all-to-all-done = bf16[32,2,1728]{2,1,0:T(2,128)(2,1)S(1)} async-done(((bf16[32,2,1728]{2,1,0:T(2,128)(2,1)}), bf16[32,2,1728]{2,1,0:T(2,128)(2,1)S(1)}, u32[]{:S(2)}, u32[]{:S(2)}) %all-to-all-start) | async-done | bytes 221216 | tf_op jit(solution)/shard_map/all_to_all | solution.py:96
  39.6 11.6 %reshape.1741 = bf16[9216,1,2,6]{3,2,1,0:T(2,128)(2,1)} reshape(bf16[32,2,1728]{2,1,0:T(2,128)(2,1)S(1)} %all-to-all-done) | data formatting | bytes 442368
  51.2 8.7 %copy.36 = bf16[2,6,1,32,288]{4,3,0,1,2:T(8,128)(2,1)S(1)} copy(bf16[2,6,1,32,288]{1,0,4,3,2:T(2,128)(2,1)} %bitcast.78) | data formatting | bytes 442368 | tf_op jit(solution)/shard_map/all_to_all | solution.py:96
  60.1 0.8 gather_fusion.2
  61.5 1.9 collective-permute-start
  63.4 8.4 %collective-permute-start.1 = (f32[2,64,1,288]{3,0,1,2:T(2,128)S(1)}, f32[2,64,1,288]{3,0,1,2:T(2,128)S(1)}, u32[]{:S(2)}, u32[]{:S(2)}) collective-permute-start(f32[2,64,1,288]{3,0,1,2:T(2,128)S(1)} %fusion.71), channel_id=1, source_target_pairs={{1,0},{2,1},{3,2},{4,3},{5,4},{6,5},{7,6},{8,7},{9,8},{10,9},{11,1... | collective-permute-start | bytes 442376 | tf_op jit(solution)/shard_map/ppermute | solution.py:19
  71.9 5.5 %collective-permute-start.3 = (f32[2,64,1,96]{3,0,1,2:T(2,128)S(1)}, f32[2,64,1,96]{3,0,1,2:T(2,128)S(1)}, u32[]{:S(2)}, u32[]{:S(2)}) collective-permute-start(f32[2,64,1,96]{3,0,1,2:T(2,128)S(1)} %get-tuple-element.67), channel_id=1, source_target_pairs={{16,0},{32,16},{48,32},{64,48},{80,64},{96,80},{112,96},{128,112},... | collective-permute-start | bytes 147464 | tf_op jit(solution)/shard_map/ppermute | solution.py:19
  77.4 1.9 collective-permute-start.2
  79.5 7.9 %collective-permute-done.2 = f32[2,64,1,96]{3,0,1,2:T(2,128)S(1)} collective-permute-done((f32[2,64,1,96]{3,0,1,2:T(2,128)S(1)}, f32[2,64,1,96]{3,0,1,2:T(2,128)S(1)}, u32[]{:S(2)}, u32[]{:S(2)}) %collective-permute-start.2) | collective-permute-done | bytes 49184 | tf_op jit(solution)/shard_map/ppermute | solution.py:19
  87.5 0.8 multiply_add_fusion.7
  89.1 1.9 collective-permute-start.4
  91.0 8.4 %collective-permute-start.5 = (f32[2,64,1,288]{3,0,1,2:T(2,128)S(1)}, f32[2,64,1,288]{3,0,1,2:T(2,128)S(1)}, u32[]{:S(2)}, u32[]{:S(2)}) collective-permute-start(f32[2,64,1,288]{3,0,1,2:T(2,128)S(1)} %broadcast_multiply_fusion), channel_id=1, source_target_pairs={{1,0},{2,1},{3,2},{4,3},{5,4},{6,5},{7,6},{8,7},{9,8},{10,9},{11,1... | collective-permute-start | bytes 442376 | tf_op jit(solution)/shard_map/ppermute | solution.py:19
  99.5 1.9 collective-permute-start.7
  101.4 3.9 %collective-permute-start.6 = (f32[2,64,1,96]{3,0,1,2:T(2,128)S(1)}, f32[2,64,1,96]{3,0,1,2:T(2,128)S(1)}, u32[]{:S(2)}, u32[]{:S(2)}) collective-permute-start(f32[2,64,1,96]{3,0,1,2:T(2,128)S(1)} %get-tuple-element.60), channel_id=1, source_target_pairs={{0,16},{16,32},{32,48},{48,64},{64,80},{80,96},{96,112},{112,128},... | collective-permute-start | bytes 147464 | tf_op jit(solution)/shard_map/ppermute | solution.py:19
  105.6 5.8 %collective-permute-done.6 = f32[2,64,1,96]{3,0,1,2:T(2,128)S(1)} collective-permute-done((f32[2,64,1,96]{3,0,1,2:T(2,128)S(1)}, f32[2,64,1,96]{3,0,1,2:T(2,128)S(1)}, u32[]{:S(2)}, u32[]{:S(2)}) %collective-permute-start.6) | collective-permute-done | bytes 49184 | tf_op jit(solution)/shard_map/ppermute | solution.py:19
  111.5 0.7 multiply_add_fusion.6
  113.1 1.9 collective-permute-start.8
  115.1 8.4 %collective-permute-start.9 = (f32[2,64,1,288]{3,0,1,2:T(2,128)S(1)}, f32[2,64,1,288]{3,0,1,2:T(2,128)S(1)}, u32[]{:S(2)}, u32[]{:S(2)}) collective-permute-start(f32[2,64,1,288]{3,0,1,2:T(2,128)S(1)} %fusion.9), channel_id=1, source_target_pairs={{1,0},{2,1},{3,2},{4,3},{5,4},{6,5},{7,6},{8,7},{9,8},{10,9},{11,1... | collective-permute-start | bytes 442376 | tf_op jit(solution)/shard_map/ppermute | solution.py:19
  123.5 1.9 collective-permute-start.11
  125.4 4.1 %collective-permute-start.10 = (f32[2,64,1,96]{3,0,1,2:T(2,128)S(1)}, f32[2,64,1,96]{3,0,1,2:T(2,128)S(1)}, u32[]{:S(2)}, u32[]{:S(2)}) collective-permute-start(f32[2,64,1,96]{3,0,1,2:T(2,128)S(1)} %get-tuple-element.54), channel_id=1, source_target_pairs={{0,16},{16,32},{32,48},{48,64},{64,80},{80,96},{96,112},{112,128},... | collective-permute-start | bytes 147464 | tf_op jit(solution)/shard_map/ppermute | solution.py:19
  129.8 0.6 collective-permute-done.11
  130.4 5.3 %collective-permute-done.10 = f32[2,64,1,96]{3,0,1,2:T(2,128)S(1)} collective-permute-done((f32[2,64,1,96]{3,0,1,2:T(2,128)S(1)}, f32[2,64,1,96]{3,0,1,2:T(2,128)S(1)}, u32[]{:S(2)}, u32[]{:S(2)}) %collective-permute-start.10) | collective-permute-done | bytes 49184 | tf_op jit(solution)/shard_map/ppermute | solution.py:19
  135.7 0.9 multiply_add_fusion.5
  137.7 1.9 collective-permute-start.12
  139.6 8.4 %collective-permute-start.13 = (f32[2,64,1,288]{3,0,1,2:T(2,128)S(1)}, f32[2,64,1,288]{3,0,1,2:T(2,128)S(1)}, u32[]{:S(2)}, u32[]{:S(2)}) collective-permute-start(f32[2,64,1,288]{3,0,1,2:T(2,128)S(1)} %fusion.14), channel_id=1, source_target_pairs={{1,0},{2,1},{3,2},{4,3},{5,4},{6,5},{7,6},{8,7},{9,8},{10,9},{11,1... | collective-permute-start | bytes 442376 | tf_op jit(solution)/shard_map/ppermute | solution.py:19
  148.1 1.9 collective-permute-start.15
  150.0 3.9 %collective-permute-start.14 = (f32[2,64,1,96]{3,0,1,2:T(2,128)S(1)}, f32[2,64,1,96]{3,0,1,2:T(2,128)S(1)}, u32[]{:S(2)}, u32[]{:S(2)}) collective-permute-start(f32[2,64,1,96]{3,0,1,2:T(2,128)S(1)} %get-tuple-element.48), channel_id=1, source_target_pairs={{0,16},{16,32},{32,48},{48,64},{64,80},{80,96},{96,112},{112,128},... | collective-permute-start | bytes 147464 | tf_op jit(solution)/shard_map/ppermute | solution.py:19
  154.2 5.8 %collective-permute-done.14 = f32[2,64,1,96]{3,0,1,2:T(2,128)S(1)} collective-permute-done((f32[2,64,1,96]{3,0,1,2:T(2,128)S(1)}, f32[2,64,1,96]{3,0,1,2:T(2,128)S(1)}, u32[]{:S(2)}, u32[]{:S(2)}) %collective-permute-start.14) | collective-permute-done | bytes 49184 | tf_op jit(solution)/shard_map/ppermute | solution.py:19
  160.1 0.9 multiply_add_fusion.4
  162.2 1.9 collective-permute-start.16
  164.1 8.4 %collective-permute-start.17 = (f32[2,64,1,288]{3,0,1,2:T(2,128)S(1)}, f32[2,64,1,288]{3,0,1,2:T(2,128)S(1)}, u32[]{:S(2)}, u32[]{:S(2)}) collective-permute-start(f32[2,64,1,288]{3,0,1,2:T(2,128)S(1)} %fusion.19), channel_id=1, source_target_pairs={{1,0},{2,1},{3,2},{4,3},{5,4},{6,5},{7,6},{8,7},{9,8},{10,9},{11,1... | collective-permute-start | bytes 442376 | tf_op jit(solution)/shard_map/ppermute | solution.py:19
  172.5 1.9 collective-permute-start.19
  174.5 3.9 %collective-permute-start.18 = (f32[2,64,1,96]{3,0,1,2:T(2,128)S(1)}, f32[2,64,1,96]{3,0,1,2:T(2,128)S(1)}, u32[]{:S(2)}, u32[]{:S(2)}) collective-permute-start(f32[2,64,1,96]{3,0,1,2:T(2,128)S(1)} %get-tuple-element.42), channel_id=1, source_target_pairs={{0,16},{16,32},{32,48},{48,64},{64,80},{80,96},{96,112},{112,128},... | collective-permute-start | bytes 147464 | tf_op jit(solution)/shard_map/ppermute | solution.py:19
  178.7 5.8 %collective-permute-done.18 = f32[2,64,1,96]{3,0,1,2:T(2,128)S(1)} collective-permute-done((f32[2,64,1,96]{3,0,1,2:T(2,128)S(1)}, f32[2,64,1,96]{3,0,1,2:T(2,128)S(1)}, u32[]{:S(2)}, u32[]{:S(2)}) %collective-permute-start.18) | collective-permute-done | bytes 49184 | tf_op jit(solution)/shard_map/ppermute | solution.py:19
  184.5 1.1 multiply_add_fusion.3
  186.9 1.9 collective-permute-start.20
  188.9 8.4 %collective-permute-start.21 = (f32[2,64,1,288]{3,0,1,2:T(2,128)S(1)}, f32[2,64,1,288]{3,0,1,2:T(2,128)S(1)}, u32[]{:S(2)}, u32[]{:S(2)}) collective-permute-start(f32[2,64,1,288]{3,0,1,2:T(2,128)S(1)} %fusion.24), channel_id=1, source_target_pairs={{1,0},{2,1},{3,2},{4,3},{5,4},{6,5},{7,6},{8,7},{9,8},{10,9},{11,1... | collective-permute-start | bytes 442376 | tf_op jit(solution)/shard_map/ppermute | solution.py:19
  197.3 1.9 collective-permute-start.23
  199.2 3.9 %collective-permute-start.22 = (f32[2,64,1,96]{3,0,1,2:T(2,128)S(1)}, f32[2,64,1,96]{3,0,1,2:T(2,128)S(1)}, u32[]{:S(2)}, u32[]{:S(2)}) collective-permute-start(f32[2,64,1,96]{3,0,1,2:T(2,128)S(1)} %get-tuple-element.36), channel_id=1, source_target_pairs={{0,16},{16,32},{32,48},{48,64},{64,80},{80,96},{96,112},{112,128},... | collective-permute-start | bytes 147464 | tf_op jit(solution)/shard_map/ppermute | solution.py:19
  203.5 5.9 %collective-permute-done.22 = f32[2,64,1,96]{3,0,1,2:T(2,128)S(1)} collective-permute-done((f32[2,64,1,96]{3,0,1,2:T(2,128)S(1)}, f32[2,64,1,96]{3,0,1,2:T(2,128)S(1)}, u32[]{:S(2)}, u32[]{:S(2)}) %collective-permute-start.22) | collective-permute-done | bytes 49184 | tf_op jit(solution)/shard_map/ppermute | solution.py:19
  209.4 1.1 multiply_add_fusion.2
  210.8 0.7 fusion.29
  211.9 1.9 collective-permute-start.24
  213.8 8.4 %collective-permute-start.25 = (f32[2,64,1,288]{3,0,1,2:T(2,128)S(1)}, f32[2,64,1,288]{3,0,1,2:T(2,128)S(1)}, u32[]{:S(2)}, u32[]{:S(2)}) collective-permute-start(f32[2,64,1,288]{3,0,1,2:T(2,128)S(1)} %fusion.29), channel_id=1, source_target_pairs={{1,0},{2,1},{3,2},{4,3},{5,4},{6,5},{7,6},{8,7},{9,8},{10,9},{11,1... | collective-permute-start | bytes 442376 | tf_op jit(solution)/shard_map/ppermute | solution.py:19
  222.3 1.9 collective-permute-start.27
  224.2 4.1 %collective-permute-start.26 = (f32[2,64,1,96]{3,0,1,2:T(2,128)S(1)}, f32[2,64,1,96]{3,0,1,2:T(2,128)S(1)}, u32[]{:S(2)}, u32[]{:S(2)}) collective-permute-start(f32[2,64,1,96]{3,0,1,2:T(2,128)S(1)} %get-tuple-element.30), channel_id=1, source_target_pairs={{0,16},{16,32},{32,48},{48,64},{64,80},{80,96},{96,112},{112,128},... | collective-permute-start | bytes 147464 | tf_op jit(solution)/shard_map/ppermute | solution.py:19
  228.6 5.8 %collective-permute-done.26 = f32[2,64,1,96]{3,0,1,2:T(2,128)S(1)} collective-permute-done((f32[2,64,1,96]{3,0,1,2:T(2,128)S(1)}, f32[2,64,1,96]{3,0,1,2:T(2,128)S(1)}, u32[]{:S(2)}, u32[]{:S(2)}) %collective-permute-start.26) | collective-permute-done | bytes 49184 | tf_op jit(solution)/shard_map/ppermute | solution.py:19
  234.4 1.3 multiply_add_fusion.1
  235.9 0.8 fusion.34
  237.1 1.9 collective-permute-start.28
  239.0 8.4 %collective-permute-start.29 = (f32[2,64,1,288]{3,0,1,2:T(2,128)S(1)}, f32[2,64,1,288]{3,0,1,2:T(2,128)S(1)}, u32[]{:S(2)}, u32[]{:S(2)}) collective-permute-start(f32[2,64,1,288]{3,0,1,2:T(2,128)S(1)} %fusion.34), channel_id=1, source_target_pairs={{1,0},{2,1},{3,2},{4,3},{5,4},{6,5},{7,6},{8,7},{9,8},{10,9},{11,1... | collective-permute-start | bytes 442376 | tf_op jit(solution)/shard_map/ppermute | solution.py:19
  247.5 1.9 collective-permute-start.31
  249.4 3.9 %collective-permute-start.30 = (f32[2,64,1,96]{3,0,1,2:T(2,128)S(1)}, f32[2,64,1,96]{3,0,1,2:T(2,128)S(1)}, u32[]{:S(2)}, u32[]{:S(2)}) collective-permute-start(f32[2,64,1,96]{3,0,1,2:T(2,128)S(1)} %get-tuple-element.24), channel_id=1, source_target_pairs={{0,16},{16,32},{32,48},{48,64},{64,80},{80,96},{96,112},{112,128},... | collective-permute-start | bytes 147464 | tf_op jit(solution)/shard_map/ppermute | solution.py:19
  253.7 5.8 %collective-permute-done.30 = f32[2,64,1,96]{3,0,1,2:T(2,128)S(1)} collective-permute-done((f32[2,64,1,96]{3,0,1,2:T(2,128)S(1)}, f32[2,64,1,96]{3,0,1,2:T(2,128)S(1)}, u32[]{:S(2)}, u32[]{:S(2)}) %collective-permute-start.30) | collective-permute-done | bytes 49184 | tf_op jit(solution)/shard_map/ppermute | solution.py:19
  259.5 1.3 multiply_add_fusion
  261.1 2.5 fusion.41
  265.0 1.3 multiply_subtract_fusion
  (93 shorter events, 11.8 us)
Async XLA Ops:
  0.6 32.7 %copy-start = (s32[1,9216]{1,0:T(1,128)S(1)}, s32[1,9216]{1,0:T(1,128)}, u32[]{:S(2)}) copy-start(s32[1,9216]{1,0:T(1,128)} %param.14) | copy-start | bytes 110596
  0.6 31.4 %copy-start.3 = (s32[32]{0:T(128)S(1)}, s32[32]{0:T(128)}, u32[]{:S(2)}) copy-start(s32[32]{0:T(128)} %param.10) | copy-start | bytes 388
  0.7 31.9 %copy-start.1 = (f32[192]{0:T(256)S(1)}, f32[192]{0:T(256)}, u32[]{:S(2)}) copy-start(f32[192]{0:T(256)} %param.12) | copy-start | bytes 2308
  0.7 33.6 %copy-start.2 = (s32[192]{0:T(256)S(1)}, s32[192]{0:T(256)}, u32[]{:S(2)}) copy-start(s32[192]{0:T(256)} %param.11) | copy-start | bytes 2308
  0.7 34.4 %copy-start.4 = (f32[16,9]{1,0:T(8,128)S(1)}, f32[16,9]{1,0:T(8,128)}, u32[]{:S(2)}) copy-start(f32[16,9]{1,0:T(8,128)} %param.13) | copy-start | bytes 1732
  0.7 34.6 %copy-start.5 = (f32[32]{0:T(128)S(1)}, f32[32]{0:T(128)}, u32[]{:S(2)}) copy-start(f32[32]{0:T(128)} %param.15) | copy-start | bytes 388
  21.6 18.0 %all-to-all-start = ((bf16[32,2,1728]{2,1,0:T(2,128)(2,1)}), bf16[32,2,1728]{2,1,0:T(2,128)(2,1)S(1)}, u32[]{:S(2)}, u32[]{:S(2)}) async-start(bf16[32,2,1728]{2,1,0:T(2,128)(2,1)} %reshape.1740), calls=%async_computation | async-start | bytes 458752 | tf_op jit(solution)/shard_map/all_to_all | solution.py:96
  61.5 25.9 %collective-permute-start = (f32[2,64,1,288]{3,0,1,2:T(2,128)S(1)}, f32[2,64,1,288]{3,0,1,2:T(2,128)S(1)}, u32[]{:S(2)}, u32[]{:S(2)}) collective-permute-start(f32[2,64,1,288]{3,0,1,2:T(2,128)S(1)} %fusion.71), channel_id=1, source_target_pairs={{0,1},{1,2},{2,3},{3,4},{4,5},{5,6},{6,7},{7,8},{8,9},{9,10},{10,1... | collective-permute-start | bytes 442376 | tf_op jit(solution)/shard_map/ppermute | solution.py:19
  63.4 24.0 %collective-permute-start.1 = (f32[2,64,1,288]{3,0,1,2:T(2,128)S(1)}, f32[2,64,1,288]{3,0,1,2:T(2,128)S(1)}, u32[]{:S(2)}, u32[]{:S(2)}) collective-permute-start(f32[2,64,1,288]{3,0,1,2:T(2,128)S(1)} %fusion.71), channel_id=1, source_target_pairs={{1,0},{2,1},{3,2},{4,3},{5,4},{6,5},{7,6},{8,7},{9,8},{10,9},{11,1... | collective-permute-start | bytes 442376 | tf_op jit(solution)/shard_map/ppermute | solution.py:19
  71.9 7.6 %collective-permute-start.3 = (f32[2,64,1,96]{3,0,1,2:T(2,128)S(1)}, f32[2,64,1,96]{3,0,1,2:T(2,128)S(1)}, u32[]{:S(2)}, u32[]{:S(2)}) collective-permute-start(f32[2,64,1,96]{3,0,1,2:T(2,128)S(1)} %get-tuple-element.67), channel_id=1, source_target_pairs={{16,0},{32,16},{48,32},{64,48},{80,64},{96,80},{112,96},{128,112},... | collective-permute-start | bytes 147464 | tf_op jit(solution)/shard_map/ppermute | solution.py:19
  77.4 10.1 %collective-permute-start.2 = (f32[2,64,1,96]{3,0,1,2:T(2,128)S(1)}, f32[2,64,1,96]{3,0,1,2:T(2,128)S(1)}, u32[]{:S(2)}, u32[]{:S(2)}) collective-permute-start(f32[2,64,1,96]{3,0,1,2:T(2,128)S(1)} %get-tuple-element.66), channel_id=1, source_target_pairs={{0,16},{16,32},{32,48},{48,64},{64,80},{80,96},{96,112},{112,128},... | collective-permute-start | bytes 147464 | tf_op jit(solution)/shard_map/ppermute | solution.py:19
  89.1 22.4 %collective-permute-start.4 = (f32[2,64,1,288]{3,0,1,2:T(2,128)S(1)}, f32[2,64,1,288]{3,0,1,2:T(2,128)S(1)}, u32[]{:S(2)}, u32[]{:S(2)}) collective-permute-start(f32[2,64,1,288]{3,0,1,2:T(2,128)S(1)} %broadcast_multiply_fusion), channel_id=1, source_target_pairs={{0,1},{1,2},{2,3},{3,4},{4,5},{5,6},{6,7},{7,8},{8,9},{9,10},{10,1... | collective-permute-start | bytes 442376 | tf_op jit(solution)/shard_map/ppermute | solution.py:19
  91.0 20.5 %collective-permute-start.5 = (f32[2,64,1,288]{3,0,1,2:T(2,128)S(1)}, f32[2,64,1,288]{3,0,1,2:T(2,128)S(1)}, u32[]{:S(2)}, u32[]{:S(2)}) collective-permute-start(f32[2,64,1,288]{3,0,1,2:T(2,128)S(1)} %broadcast_multiply_fusion), channel_id=1, source_target_pairs={{1,0},{2,1},{3,2},{4,3},{5,4},{6,5},{7,6},{8,7},{9,8},{10,9},{11,1... | collective-permute-start | bytes 442376 | tf_op jit(solution)/shard_map/ppermute | solution.py:19
  99.5 6.2 %collective-permute-start.7 = (f32[2,64,1,96]{3,0,1,2:T(2,128)S(1)}, f32[2,64,1,96]{3,0,1,2:T(2,128)S(1)}, u32[]{:S(2)}, u32[]{:S(2)}) collective-permute-start(f32[2,64,1,96]{3,0,1,2:T(2,128)S(1)} %get-tuple-element.61), channel_id=1, source_target_pairs={{16,0},{32,16},{48,32},{64,48},{80,64},{96,80},{112,96},{128,112},... | collective-permute-start | bytes 147464 | tf_op jit(solution)/shard_map/ppermute | solution.py:19
  101.4 10.1 %collective-permute-start.6 = (f32[2,64,1,96]{3,0,1,2:T(2,128)S(1)}, f32[2,64,1,96]{3,0,1,2:T(2,128)S(1)}, u32[]{:S(2)}, u32[]{:S(2)}) collective-permute-start(f32[2,64,1,96]{3,0,1,2:T(2,128)S(1)} %get-tuple-element.60), channel_id=1, source_target_pairs={{0,16},{16,32},{32,48},{48,64},{64,80},{80,96},{96,112},{112,128},... | collective-permute-start | bytes 147464 | tf_op jit(solution)/shard_map/ppermute | solution.py:19
  113.1 22.6 %collective-permute-start.8 = (f32[2,64,1,288]{3,0,1,2:T(2,128)S(1)}, f32[2,64,1,288]{3,0,1,2:T(2,128)S(1)}, u32[]{:S(2)}, u32[]{:S(2)}) collective-permute-start(f32[2,64,1,288]{3,0,1,2:T(2,128)S(1)} %fusion.9), channel_id=1, source_target_pairs={{0,1},{1,2},{2,3},{3,4},{4,5},{5,6},{6,7},{7,8},{8,9},{9,10},{10,1... | collective-permute-start | bytes 442376 | tf_op jit(solution)/shard_map/ppermute | solution.py:19
  115.1 20.6 %collective-permute-start.9 = (f32[2,64,1,288]{3,0,1,2:T(2,128)S(1)}, f32[2,64,1,288]{3,0,1,2:T(2,128)S(1)}, u32[]{:S(2)}, u32[]{:S(2)}) collective-permute-start(f32[2,64,1,288]{3,0,1,2:T(2,128)S(1)} %fusion.9), channel_id=1, source_target_pairs={{1,0},{2,1},{3,2},{4,3},{5,4},{6,5},{7,6},{8,7},{9,8},{10,9},{11,1... | collective-permute-start | bytes 442376 | tf_op jit(solution)/shard_map/ppermute | solution.py:19
  123.5 6.9 %collective-permute-start.11 = (f32[2,64,1,96]{3,0,1,2:T(2,128)S(1)}, f32[2,64,1,96]{3,0,1,2:T(2,128)S(1)}, u32[]{:S(2)}, u32[]{:S(2)}) collective-permute-start(f32[2,64,1,96]{3,0,1,2:T(2,128)S(1)} %get-tuple-element.55), channel_id=1, source_target_pairs={{16,0},{32,16},{48,32},{64,48},{80,64},{96,80},{112,96},{128,112},... | collective-permute-start | bytes 147464 | tf_op jit(solution)/shard_map/ppermute | solution.py:19
  125.4 10.2 %collective-permute-start.10 = (f32[2,64,1,96]{3,0,1,2:T(2,128)S(1)}, f32[2,64,1,96]{3,0,1,2:T(2,128)S(1)}, u32[]{:S(2)}, u32[]{:S(2)}) collective-permute-start(f32[2,64,1,96]{3,0,1,2:T(2,128)S(1)} %get-tuple-element.54), channel_id=1, source_target_pairs={{0,16},{16,32},{32,48},{48,64},{64,80},{80,96},{96,112},{112,128},... | collective-permute-start | bytes 147464 | tf_op jit(solution)/shard_map/ppermute | solution.py:19
  137.7 22.4 %collective-permute-start.12 = (f32[2,64,1,288]{3,0,1,2:T(2,128)S(1)}, f32[2,64,1,288]{3,0,1,2:T(2,128)S(1)}, u32[]{:S(2)}, u32[]{:S(2)}) collective-permute-start(f32[2,64,1,288]{3,0,1,2:T(2,128)S(1)} %fusion.14), channel_id=1, source_target_pairs={{0,1},{1,2},{2,3},{3,4},{4,5},{5,6},{6,7},{7,8},{8,9},{9,10},{10,1... | collective-permute-start | bytes 442376 | tf_op jit(solution)/shard_map/ppermute | solution.py:19
  139.6 20.5 %collective-permute-start.13 = (f32[2,64,1,288]{3,0,1,2:T(2,128)S(1)}, f32[2,64,1,288]{3,0,1,2:T(2,128)S(1)}, u32[]{:S(2)}, u32[]{:S(2)}) collective-permute-start(f32[2,64,1,288]{3,0,1,2:T(2,128)S(1)} %fusion.14), channel_id=1, source_target_pairs={{1,0},{2,1},{3,2},{4,3},{5,4},{6,5},{7,6},{8,7},{9,8},{10,9},{11,1... | collective-permute-start | bytes 442376 | tf_op jit(solution)/shard_map/ppermute | solution.py:19
  148.1 6.2 %collective-permute-start.15 = (f32[2,64,1,96]{3,0,1,2:T(2,128)S(1)}, f32[2,64,1,96]{3,0,1,2:T(2,128)S(1)}, u32[]{:S(2)}, u32[]{:S(2)}) collective-permute-start(f32[2,64,1,96]{3,0,1,2:T(2,128)S(1)} %get-tuple-element.49), channel_id=1, source_target_pairs={{16,0},{32,16},{48,32},{64,48},{80,64},{96,80},{112,96},{128,112},... | collective-permute-start | bytes 147464 | tf_op jit(solution)/shard_map/ppermute | solution.py:19
  150.0 10.1 %collective-permute-start.14 = (f32[2,64,1,96]{3,0,1,2:T(2,128)S(1)}, f32[2,64,1,96]{3,0,1,2:T(2,128)S(1)}, u32[]{:S(2)}, u32[]{:S(2)}) collective-permute-start(f32[2,64,1,96]{3,0,1,2:T(2,128)S(1)} %get-tuple-element.48), channel_id=1, source_target_pairs={{0,16},{16,32},{32,48},{48,64},{64,80},{80,96},{96,112},{112,128},... | collective-permute-start | bytes 147464 | tf_op jit(solution)/shard_map/ppermute | solution.py:19
  162.2 22.4 %collective-permute-start.16 = (f32[2,64,1,288]{3,0,1,2:T(2,128)S(1)}, f32[2,64,1,288]{3,0,1,2:T(2,128)S(1)}, u32[]{:S(2)}, u32[]{:S(2)}) collective-permute-start(f32[2,64,1,288]{3,0,1,2:T(2,128)S(1)} %fusion.19), channel_id=1, source_target_pairs={{0,1},{1,2},{2,3},{3,4},{4,5},{5,6},{6,7},{7,8},{8,9},{9,10},{10,1... | collective-permute-start | bytes 442376 | tf_op jit(solution)/shard_map/ppermute | solution.py:19
  164.1 20.5 %collective-permute-start.17 = (f32[2,64,1,288]{3,0,1,2:T(2,128)S(1)}, f32[2,64,1,288]{3,0,1,2:T(2,128)S(1)}, u32[]{:S(2)}, u32[]{:S(2)}) collective-permute-start(f32[2,64,1,288]{3,0,1,2:T(2,128)S(1)} %fusion.19), channel_id=1, source_target_pairs={{1,0},{2,1},{3,2},{4,3},{5,4},{6,5},{7,6},{8,7},{9,8},{10,9},{11,1... | collective-permute-start | bytes 442376 | tf_op jit(solution)/shard_map/ppermute | solution.py:19
  172.5 6.2 %collective-permute-start.19 = (f32[2,64,1,96]{3,0,1,2:T(2,128)S(1)}, f32[2,64,1,96]{3,0,1,2:T(2,128)S(1)}, u32[]{:S(2)}, u32[]{:S(2)}) collective-permute-start(f32[2,64,1,96]{3,0,1,2:T(2,128)S(1)} %get-tuple-element.43), channel_id=1, source_target_pairs={{16,0},{32,16},{48,32},{64,48},{80,64},{96,80},{112,96},{128,112},... | collective-permute-start | bytes 147464 | tf_op jit(solution)/shard_map/ppermute | solution.py:19
  174.5 10.1 %collective-permute-start.18 = (f32[2,64,1,96]{3,0,1,2:T(2,128)S(1)}, f32[2,64,1,96]{3,0,1,2:T(2,128)S(1)}, u32[]{:S(2)}, u32[]{:S(2)}) collective-permute-start(f32[2,64,1,96]{3,0,1,2:T(2,128)S(1)} %get-tuple-element.42), channel_id=1, source_target_pairs={{0,16},{16,32},{32,48},{48,64},{64,80},{80,96},{96,112},{112,128},... | collective-permute-start | bytes 147464 | tf_op jit(solution)/shard_map/ppermute | solution.py:19
  186.9 22.5 %collective-permute-start.20 = (f32[2,64,1,288]{3,0,1,2:T(2,128)S(1)}, f32[2,64,1,288]{3,0,1,2:T(2,128)S(1)}, u32[]{:S(2)}, u32[]{:S(2)}) collective-permute-start(f32[2,64,1,288]{3,0,1,2:T(2,128)S(1)} %fusion.24), channel_id=1, source_target_pairs={{0,1},{1,2},{2,3},{3,4},{4,5},{5,6},{6,7},{7,8},{8,9},{9,10},{10,1... | collective-permute-start | bytes 442376 | tf_op jit(solution)/shard_map/ppermute | solution.py:19
  188.9 20.6 %collective-permute-start.21 = (f32[2,64,1,288]{3,0,1,2:T(2,128)S(1)}, f32[2,64,1,288]{3,0,1,2:T(2,128)S(1)}, u32[]{:S(2)}, u32[]{:S(2)}) collective-permute-start(f32[2,64,1,288]{3,0,1,2:T(2,128)S(1)} %fusion.24), channel_id=1, source_target_pairs={{1,0},{2,1},{3,2},{4,3},{5,4},{6,5},{7,6},{8,7},{9,8},{10,9},{11,1... | collective-permute-start | bytes 442376 | tf_op jit(solution)/shard_map/ppermute | solution.py:19
  197.3 6.2 %collective-permute-start.23 = (f32[2,64,1,96]{3,0,1,2:T(2,128)S(1)}, f32[2,64,1,96]{3,0,1,2:T(2,128)S(1)}, u32[]{:S(2)}, u32[]{:S(2)}) collective-permute-start(f32[2,64,1,96]{3,0,1,2:T(2,128)S(1)} %get-tuple-element.37), channel_id=1, source_target_pairs={{16,0},{32,16},{48,32},{64,48},{80,64},{96,80},{112,96},{128,112},... | collective-permute-start | bytes 147464 | tf_op jit(solution)/shard_map/ppermute | solution.py:19
  199.2 10.2 %collective-permute-start.22 = (f32[2,64,1,96]{3,0,1,2:T(2,128)S(1)}, f32[2,64,1,96]{3,0,1,2:T(2,128)S(1)}, u32[]{:S(2)}, u32[]{:S(2)}) collective-permute-start(f32[2,64,1,96]{3,0,1,2:T(2,128)S(1)} %get-tuple-element.36), channel_id=1, source_target_pairs={{0,16},{16,32},{32,48},{48,64},{64,80},{80,96},{96,112},{112,128},... | collective-permute-start | bytes 147464 | tf_op jit(solution)/shard_map/ppermute | solution.py:19
  211.9 22.5 %collective-permute-start.24 = (f32[2,64,1,288]{3,0,1,2:T(2,128)S(1)}, f32[2,64,1,288]{3,0,1,2:T(2,128)S(1)}, u32[]{:S(2)}, u32[]{:S(2)}) collective-permute-start(f32[2,64,1,288]{3,0,1,2:T(2,128)S(1)} %fusion.29), channel_id=1, source_target_pairs={{0,1},{1,2},{2,3},{3,4},{4,5},{5,6},{6,7},{7,8},{8,9},{9,10},{10,1... | collective-permute-start | bytes 442376 | tf_op jit(solution)/shard_map/ppermute | solution.py:19
  213.8 20.6 %collective-permute-start.25 = (f32[2,64,1,288]{3,0,1,2:T(2,128)S(1)}, f32[2,64,1,288]{3,0,1,2:T(2,128)S(1)}, u32[]{:S(2)}, u32[]{:S(2)}) collective-permute-start(f32[2,64,1,288]{3,0,1,2:T(2,128)S(1)} %fusion.29), channel_id=1, source_target_pairs={{1,0},{2,1},{3,2},{4,3},{5,4},{6,5},{7,6},{8,7},{9,8},{10,9},{11,1... | collective-permute-start | bytes 442376 | tf_op jit(solution)/shard_map/ppermute | solution.py:19
  222.3 6.3 %collective-permute-start.27 = (f32[2,64,1,96]{3,0,1,2:T(2,128)S(1)}, f32[2,64,1,96]{3,0,1,2:T(2,128)S(1)}, u32[]{:S(2)}, u32[]{:S(2)}) collective-permute-start(f32[2,64,1,96]{3,0,1,2:T(2,128)S(1)} %get-tuple-element.31), channel_id=1, source_target_pairs={{16,0},{32,16},{48,32},{64,48},{80,64},{96,80},{112,96},{128,112},... | collective-permute-start | bytes 147464 | tf_op jit(solution)/shard_map/ppermute | solution.py:19
  224.2 10.2 %collective-permute-start.26 = (f32[2,64,1,96]{3,0,1,2:T(2,128)S(1)}, f32[2,64,1,96]{3,0,1,2:T(2,128)S(1)}, u32[]{:S(2)}, u32[]{:S(2)}) collective-permute-start(f32[2,64,1,96]{3,0,1,2:T(2,128)S(1)} %get-tuple-element.30), channel_id=1, source_target_pairs={{0,16},{16,32},{32,48},{48,64},{64,80},{80,96},{96,112},{112,128},... | collective-permute-start | bytes 147464 | tf_op jit(solution)/shard_map/ppermute | solution.py:19
  237.1 22.4 %collective-permute-start.28 = (f32[2,64,1,288]{3,0,1,2:T(2,128)S(1)}, f32[2,64,1,288]{3,0,1,2:T(2,128)S(1)}, u32[]{:S(2)}, u32[]{:S(2)}) collective-permute-start(f32[2,64,1,288]{3,0,1,2:T(2,128)S(1)} %fusion.34), channel_id=1, source_target_pairs={{0,1},{1,2},{2,3},{3,4},{4,5},{5,6},{6,7},{7,8},{8,9},{9,10},{10,1... | collective-permute-start | bytes 442376 | tf_op jit(solution)/shard_map/ppermute | solution.py:19
  239.0 20.5 %collective-permute-start.29 = (f32[2,64,1,288]{3,0,1,2:T(2,128)S(1)}, f32[2,64,1,288]{3,0,1,2:T(2,128)S(1)}, u32[]{:S(2)}, u32[]{:S(2)}) collective-permute-start(f32[2,64,1,288]{3,0,1,2:T(2,128)S(1)} %fusion.34), channel_id=1, source_target_pairs={{1,0},{2,1},{3,2},{4,3},{5,4},{6,5},{7,6},{8,7},{9,8},{10,9},{11,1... | collective-permute-start | bytes 442376 | tf_op jit(solution)/shard_map/ppermute | solution.py:19
  247.5 6.2 %collective-permute-start.31 = (f32[2,64,1,96]{3,0,1,2:T(2,128)S(1)}, f32[2,64,1,96]{3,0,1,2:T(2,128)S(1)}, u32[]{:S(2)}, u32[]{:S(2)}) collective-permute-start(f32[2,64,1,96]{3,0,1,2:T(2,128)S(1)} %get-tuple-element.25), channel_id=1, source_target_pairs={{16,0},{32,16},{48,32},{64,48},{80,64},{96,80},{112,96},{128,112},... | collective-permute-start | bytes 147464 | tf_op jit(solution)/shard_map/ppermute | solution.py:19
  249.4 10.1 %collective-permute-start.30 = (f32[2,64,1,96]{3,0,1,2:T(2,128)S(1)}, f32[2,64,1,96]{3,0,1,2:T(2,128)S(1)}, u32[]{:S(2)}, u32[]{:S(2)}) collective-permute-start(f32[2,64,1,96]{3,0,1,2:T(2,128)S(1)} %get-tuple-element.24), channel_id=1, source_target_pairs={{0,16},{16,32},{32,48},{48,64},{64,80},{80,96},{96,112},{112,128},... | collective-permute-start | bytes 147464 | tf_op jit(solution)/shard_map/ppermute | solution.py:19
where the time goes:
time: 268 us; the launch traced here: 266 us
  starting transfers between devices  142 us (53%)
  waiting for transfers between devices  52.9 us (20%)
  local copies, waits for them, and re-layouts  50.7 us (19%)
  other arithmetic  18.3 us (7%)
    ppermute x32, starting transfers between devices, shifted(): return lax.ppermute(shard, axis, pairs)  132 us
    ppermute x32, waiting for transfers between devices, shifted(): return lax.ppermute(shard, axis, pairs)  49.5 us
    unnamed x15, local copies, waits for them, and re-layouts  32.5 us
    all_to_all x1, starting transfers between devices, body(): lax.all_to_all(quasi, 'cuts', split_axis=3, concat_axis=1, tiled=True)  10.4 us
    all_to_all x2, local copies, waits for them, and re-layouts, body(): lax.all_to_all(quasi, 'cuts', split_axis=3, concat_axis=1, tiled=True)  8.98 us
    add x8, other arithmetic, combine(): single = 0.5 * (6.0 * field - beside_all) + potential * field  8.3 us
  transfers between devices with their start and end apart: 33, of which 15 were waited for; matrix products, arithmetic and copies ran while one was open for 2% of the time, Pallas kernels for 0%

commit v1 on v0

--- a/solution.py
+++ b/solution.py
@@ -2,6 +2,7 @@
 import jax.numpy as jnp
 from jax import lax
 from jax.sharding import PartitionSpec as P
+from jax.lax import all_to_all, axis_size
 
 NX = 96
 VEC_DEV = 2
@@ -93,7 +94,9 @@
     pairing_local = lax.dynamic_slice_in_dim(pairing, offset, share, 1)
     index_local = lax.dynamic_slice_in_dim(trap_index, offset, share, 1)
     potential = trap_lookup(index_local, trap_table) + mean_local
-    moved = lax.all_to_all(quasi, "cuts", split_axis=3, concat_axis=1, tiled=True)
+    moved = jnp.concatenate(
+        all_to_all(jnp.stack(jnp.split(quasi, axis_size("cuts"), axis=3)), "cuts", 0, 0), axis=1
+    )
     total_live = VEC_DEV * cut_count
     ends = jnp.cumsum(counts)
     starts = ends - counts

time: 268 us -> 257 us (0.959)
  the two profiles are of different devices: /device:TPU:262 before, /device:TPU:222 now
where the time goes in v1:
time: 257 us; the launch traced here: 255 us
  starting transfers between devices  141 us (55%)
  waiting for transfers between devices  52.8 us (21%)
  local copies, waits for them, and re-layouts  40.5 us (16%)
  other arithmetic  18.1 us (7%)
    ppermute x32, starting transfers between devices, shifted(): return lax.ppermute(shard, axis, pairs)  130 us
    ppermute x32, waiting for transfers between devices, shifted(): return lax.ppermute(shard, axis, pairs)  49.3 us
    unnamed x45, local copies, waits for them, and re-layouts  30.6 us
    all_to_all x1, starting transfers between devices, body(): all_to_all(jnp.stack(jnp.split(quasi, axis_size('cuts'), axis=3)), 'cuts'...  11 us
    add x8, other arithmetic, combine(): single = 0.5 * (6.0 * field - beside_all) + potential * field  8.09 us
  transfers between devices with their start and end apart: 33, of which 15 were waited for; matrix products, arithmetic and copies ran while one was open for 2% of the time, Pallas kernels for 0%

profile of v1, /device:TPU:222, one launch (start us, length us, event | category | flops | bytes accessed | tf_op | source)
XLA Modules:
  0.0 255.1 jit_solution(8898536253630700100)
XLA Ops:
  0.7 1.4 constant_dynamic-update-slice_fusion.31
  2.0 1.4 constant_dynamic-update-slice_fusion.30
  3.4 1.4 constant_dynamic-update-slice_fusion.29
  4.8 1.4 constant_dynamic-update-slice_fusion.28
  6.2 1.3 constant_dynamic-update-slice_fusion.27
  7.5 1.4 constant_dynamic-update-slice_fusion.26
  8.9 1.4 constant_dynamic-update-slice_fusion.25
  10.2 1.4 constant_dynamic-update-slice_fusion.24
  11.6 1.3 constant_dynamic-update-slice_fusion.23
  12.9 1.4 constant_dynamic-update-slice_fusion.22
  14.3 1.4 constant_dynamic-update-slice_fusion.21
  15.7 1.4 constant_dynamic-update-slice_fusion.20
  30.2 11.0 %all-to-all-start = ((bf16[32,2,6,1,288]{4,1,2,3,0:T(2,128)(2,1)}), bf16[32,2,6,1,288]{4,1,2,3,0:T(2,128)(2,1)S(1)}, u32[]{:S(2)}, u32[]{:S(2)}) async-start(bf16[32,2,6,1,288]{4,1,2,3,0:T(2,128)(2,1)} %constant_dynamic-update-slice_fusion), calls=%async_computation | async-start | bytes 589824 | tf_op jit(solution)/shard_map/all_to_all | solution.py:98
  46.1 0.8 fusion
  47.0 3.5 %all-to-all-done = bf16[32,2,6,1,288]{4,1,2,3,0:T(2,128)(2,1)S(1)} async-done(((bf16[32,2,6,1,288]{4,1,2,3,0:T(2,128)(2,1)}), bf16[32,2,6,1,288]{4,1,2,3,0:T(2,128)(2,1)S(1)}, u32[]{:S(2)}, u32[]{:S(2)}) %all-to-all-start) | async-done | bytes 221216 | tf_op jit(solution)/shard_map/all_to_all | solution.py:98
  51.9 1.9 collective-permute-start
  53.8 8.4 %collective-permute-start.1 = (f32[2,64,1,288]{3,0,1,2:T(2,128)S(1)}, f32[2,64,1,288]{3,0,1,2:T(2,128)S(1)}, u32[]{:S(2)}, u32[]{:S(2)}) collective-permute-start(f32[2,64,1,288]{3,0,1,2:T(2,128)S(1)} %fusion.71), channel_id=1, source_target_pairs={{1,0},{2,1},{3,2},{4,3},{5,4},{6,5},{7,6},{8,7},{9,8},{10,9},{11,1... | collective-permute-start | bytes 442376 | tf_op jit(solution)/shard_map/ppermute | solution.py:20
  62.2 4.3 %collective-permute-start.2 = (f32[2,64,1,96]{3,0,1,2:T(2,128)S(1)}, f32[2,64,1,96]{3,0,1,2:T(2,128)S(1)}, u32[]{:S(2)}, u32[]{:S(2)}) collective-permute-start(f32[2,64,1,96]{3,0,1,2:T(2,128)S(1)} %get-tuple-element.66), channel_id=1, source_target_pairs={{0,16},{16,32},{32,48},{48,64},{64,80},{80,96},{96,112},{112,128},... | collective-permute-start | bytes 147464 | tf_op jit(solution)/shard_map/ppermute | solution.py:20
  66.5 1.9 collective-permute-start.3
  68.6 1.4 collective-permute-done.2
  70.0 6.6 %collective-permute-done.3 = f32[2,64,1,96]{3,0,1,2:T(2,128)S(1)} collective-permute-done((f32[2,64,1,96]{3,0,1,2:T(2,128)S(1)}, f32[2,64,1,96]{3,0,1,2:T(2,128)S(1)}, u32[]{:S(2)}, u32[]{:S(2)}) %collective-permute-start.3) | collective-permute-done | bytes 49184 | tf_op jit(solution)/shard_map/ppermute | solution.py:20
  78.2 1.9 collective-permute-start.4
  80.1 8.4 %collective-permute-start.5 = (f32[2,64,1,288]{3,0,1,2:T(2,128)S(1)}, f32[2,64,1,288]{3,0,1,2:T(2,128)S(1)}, u32[]{:S(2)}, u32[]{:S(2)}) collective-permute-start(f32[2,64,1,288]{3,0,1,2:T(2,128)S(1)} %broadcast_multiply_fusion), channel_id=1, source_target_pairs={{1,0},{2,1},{3,2},{4,3},{5,4},{6,5},{7,6},{8,7},{9,8},{10,9},{11,1... | collective-permute-start | bytes 442376 | tf_op jit(solution)/shard_map/ppermute | solution.py:20
  88.6 1.9 collective-permute-start.6
  90.5 3.9 %collective-permute-start.7 = (f32[2,64,1,96]{3,0,1,2:T(2,128)S(1)}, f32[2,64,1,96]{3,0,1,2:T(2,128)S(1)}, u32[]{:S(2)}, u32[]{:S(2)}) collective-permute-start(f32[2,64,1,96]{3,0,1,2:T(2,128)S(1)} %get-tuple-element.61), channel_id=1, source_target_pairs={{16,0},{32,16},{48,32},{64,48},{80,64},{96,80},{112,96},{128,112},... | collective-permute-start | bytes 147464 | tf_op jit(solution)/shard_map/ppermute | solution.py:20
  94.7 5.8 %collective-permute-done.7 = f32[2,64,1,96]{3,0,1,2:T(2,128)S(1)} collective-permute-done((f32[2,64,1,96]{3,0,1,2:T(2,128)S(1)}, f32[2,64,1,96]{3,0,1,2:T(2,128)S(1)}, u32[]{:S(2)}, u32[]{:S(2)}) %collective-permute-start.7) | collective-permute-done | bytes 49184 | tf_op jit(solution)/shard_map/ppermute | solution.py:20
  102.2 1.9 collective-permute-start.8
  104.2 8.4 %collective-permute-start.9 = (f32[2,64,1,288]{3,0,1,2:T(2,128)S(1)}, f32[2,64,1,288]{3,0,1,2:T(2,128)S(1)}, u32[]{:S(2)}, u32[]{:S(2)}) collective-permute-start(f32[2,64,1,288]{3,0,1,2:T(2,128)S(1)} %fusion.9), channel_id=1, source_target_pairs={{1,0},{2,1},{3,2},{4,3},{5,4},{6,5},{7,6},{8,7},{9,8},{10,9},{11,1... | collective-permute-start | bytes 442376 | tf_op jit(solution)/shard_map/ppermute | solution.py:20
  112.6 1.9 collective-permute-start.10
  114.5 3.9 %collective-permute-start.11 = (f32[2,64,1,96]{3,0,1,2:T(2,128)S(1)}, f32[2,64,1,96]{3,0,1,2:T(2,128)S(1)}, u32[]{:S(2)}, u32[]{:S(2)}) collective-permute-start(f32[2,64,1,96]{3,0,1,2:T(2,128)S(1)} %get-tuple-element.55), channel_id=1, source_target_pairs={{16,0},{32,16},{48,32},{64,48},{80,64},{96,80},{112,96},{128,112},... | collective-permute-start | bytes 147464 | tf_op jit(solution)/shard_map/ppermute | solution.py:20
  118.8 5.8 %collective-permute-done.11 = f32[2,64,1,96]{3,0,1,2:T(2,128)S(1)} collective-permute-done((f32[2,64,1,96]{3,0,1,2:T(2,128)S(1)}, f32[2,64,1,96]{3,0,1,2:T(2,128)S(1)}, u32[]{:S(2)}, u32[]{:S(2)}) %collective-permute-start.11) | collective-permute-done | bytes 49184 | tf_op jit(solution)/shard_map/ppermute | solution.py:20
  124.6 0.9 multiply_add_fusion.5
  126.6 1.9 collective-permute-start.12
  128.5 8.4 %collective-permute-start.13 = (f32[2,64,1,288]{3,0,1,2:T(2,128)S(1)}, f32[2,64,1,288]{3,0,1,2:T(2,128)S(1)}, u32[]{:S(2)}, u32[]{:S(2)}) collective-permute-start(f32[2,64,1,288]{3,0,1,2:T(2,128)S(1)} %fusion.14), channel_id=1, source_target_pairs={{1,0},{2,1},{3,2},{4,3},{5,4},{6,5},{7,6},{8,7},{9,8},{10,9},{11,1... | collective-permute-start | bytes 442376 | tf_op jit(solution)/shard_map/ppermute | solution.py:20
  137.0 1.9 collective-permute-start.14
  138.9 4.1 %collective-permute-start.15 = (f32[2,64,1,96]{3,0,1,2:T(2,128)S(1)}, f32[2,64,1,96]{3,0,1,2:T(2,128)S(1)}, u32[]{:S(2)}, u32[]{:S(2)}) collective-permute-start(f32[2,64,1,96]{3,0,1,2:T(2,128)S(1)} %get-tuple-element.49), channel_id=1, source_target_pairs={{16,0},{32,16},{48,32},{64,48},{80,64},{96,80},{112,96},{128,112},... | collective-permute-start | bytes 147464 | tf_op jit(solution)/shard_map/ppermute | solution.py:20
  143.2 5.7 %collective-permute-done.15 = f32[2,64,1,96]{3,0,1,2:T(2,128)S(1)} collective-permute-done((f32[2,64,1,96]{3,0,1,2:T(2,128)S(1)}, f32[2,64,1,96]{3,0,1,2:T(2,128)S(1)}, u32[]{:S(2)}, u32[]{:S(2)}) %collective-permute-start.15) | collective-permute-done | bytes 49184 | tf_op jit(solution)/shard_map/ppermute | solution.py:20
  149.0 0.9 multiply_add_fusion.4
  151.0 1.9 collective-permute-start.16
  152.9 8.4 %collective-permute-start.17 = (f32[2,64,1,288]{3,0,1,2:T(2,128)S(1)}, f32[2,64,1,288]{3,0,1,2:T(2,128)S(1)}, u32[]{:S(2)}, u32[]{:S(2)}) collective-permute-start(f32[2,64,1,288]{3,0,1,2:T(2,128)S(1)} %fusion.19), channel_id=1, source_target_pairs={{1,0},{2,1},{3,2},{4,3},{5,4},{6,5},{7,6},{8,7},{9,8},{10,9},{11,1... | collective-permute-start | bytes 442376 | tf_op jit(solution)/shard_map/ppermute | solution.py:20
  161.4 1.9 collective-permute-start.18
  163.3 3.9 %collective-permute-start.19 = (f32[2,64,1,96]{3,0,1,2:T(2,128)S(1)}, f32[2,64,1,96]{3,0,1,2:T(2,128)S(1)}, u32[]{:S(2)}, u32[]{:S(2)}) collective-permute-start(f32[2,64,1,96]{3,0,1,2:T(2,128)S(1)} %get-tuple-element.43), channel_id=1, source_target_pairs={{16,0},{32,16},{48,32},{64,48},{80,64},{96,80},{112,96},{128,112},... | collective-permute-start | bytes 147464 | tf_op jit(solution)/shard_map/ppermute | solution.py:20
  167.6 5.9 %collective-permute-done.19 = f32[2,64,1,96]{3,0,1,2:T(2,128)S(1)} collective-permute-done((f32[2,64,1,96]{3,0,1,2:T(2,128)S(1)}, f32[2,64,1,96]{3,0,1,2:T(2,128)S(1)}, u32[]{:S(2)}, u32[]{:S(2)}) %collective-permute-start.19) | collective-permute-done | bytes 49184 | tf_op jit(solution)/shard_map/ppermute | solution.py:20
  173.4 1.1 multiply_add_fusion.3
  175.8 1.9 collective-permute-start.20
  177.7 8.4 %collective-permute-start.21 = (f32[2,64,1,288]{3,0,1,2:T(2,128)S(1)}, f32[2,64,1,288]{3,0,1,2:T(2,128)S(1)}, u32[]{:S(2)}, u32[]{:S(2)}) collective-permute-start(f32[2,64,1,288]{3,0,1,2:T(2,128)S(1)} %fusion.24), channel_id=1, source_target_pairs={{1,0},{2,1},{3,2},{4,3},{5,4},{6,5},{7,6},{8,7},{9,8},{10,9},{11,1... | collective-permute-start | bytes 442376 | tf_op jit(solution)/shard_map/ppermute | solution.py:20
  186.2 1.9 collective-permute-start.22
  188.1 3.9 %collective-permute-start.23 = (f32[2,64,1,96]{3,0,1,2:T(2,128)S(1)}, f32[2,64,1,96]{3,0,1,2:T(2,128)S(1)}, u32[]{:S(2)}, u32[]{:S(2)}) collective-permute-start(f32[2,64,1,96]{3,0,1,2:T(2,128)S(1)} %get-tuple-element.37), channel_id=1, source_target_pairs={{16,0},{32,16},{48,32},{64,48},{80,64},{96,80},{112,96},{128,112},... | collective-permute-start | bytes 147464 | tf_op jit(solution)/shard_map/ppermute | solution.py:20
  192.3 5.9 %collective-permute-done.23 = f32[2,64,1,96]{3,0,1,2:T(2,128)S(1)} collective-permute-done((f32[2,64,1,96]{3,0,1,2:T(2,128)S(1)}, f32[2,64,1,96]{3,0,1,2:T(2,128)S(1)}, u32[]{:S(2)}, u32[]{:S(2)}) %collective-permute-start.23) | collective-permute-done | bytes 49184 | tf_op jit(solution)/shard_map/ppermute | solution.py:20
  198.3 1.1 multiply_add_fusion.2
  200.7 1.9 collective-permute-start.24
  202.6 8.4 %collective-permute-start.25 = (f32[2,64,1,288]{3,0,1,2:T(2,128)S(1)}, f32[2,64,1,288]{3,0,1,2:T(2,128)S(1)}, u32[]{:S(2)}, u32[]{:S(2)}) collective-permute-start(f32[2,64,1,288]{3,0,1,2:T(2,128)S(1)} %fusion.29), channel_id=1, source_target_pairs={{1,0},{2,1},{3,2},{4,3},{5,4},{6,5},{7,6},{8,7},{9,8},{10,9},{11,1... | collective-permute-start | bytes 442376 | tf_op jit(solution)/shard_map/ppermute | solution.py:20
  211.1 1.9 collective-permute-start.26
  213.0 3.9 %collective-permute-start.27 = (f32[2,64,1,96]{3,0,1,2:T(2,128)S(1)}, f32[2,64,1,96]{3,0,1,2:T(2,128)S(1)}, u32[]{:S(2)}, u32[]{:S(2)}) collective-permute-start(f32[2,64,1,96]{3,0,1,2:T(2,128)S(1)} %get-tuple-element.31), channel_id=1, source_target_pairs={{16,0},{32,16},{48,32},{64,48},{80,64},{96,80},{112,96},{128,112},... | collective-permute-start | bytes 147464 | tf_op jit(solution)/shard_map/ppermute | solution.py:20
  217.3 5.9 %collective-permute-done.27 = f32[2,64,1,96]{3,0,1,2:T(2,128)S(1)} collective-permute-done((f32[2,64,1,96]{3,0,1,2:T(2,128)S(1)}, f32[2,64,1,96]{3,0,1,2:T(2,128)S(1)}, u32[]{:S(2)}, u32[]{:S(2)}) %collective-permute-start.27) | collective-permute-done | bytes 49184 | tf_op jit(solution)/shard_map/ppermute | solution.py:20
  223.2 1.3 multiply_add_fusion.1
  225.9 1.9 collective-permute-start.28
  227.8 8.4 %collective-permute-start.29 = (f32[2,64,1,288]{3,0,1,2:T(2,128)S(1)}, f32[2,64,1,288]{3,0,1,2:T(2,128)S(1)}, u32[]{:S(2)}, u32[]{:S(2)}) collective-permute-start(f32[2,64,1,288]{3,0,1,2:T(2,128)S(1)} %fusion.34), channel_id=1, source_target_pairs={{1,0},{2,1},{3,2},{4,3},{5,4},{6,5},{7,6},{8,7},{9,8},{10,9},{11,1... | collective-permute-start | bytes 442376 | tf_op jit(solution)/shard_map/ppermute | solution.py:20
  236.3 1.9 collective-permute-start.30
  238.2 4.1 %collective-permute-start.31 = (f32[2,64,1,96]{3,0,1,2:T(2,128)S(1)}, f32[2,64,1,96]{3,0,1,2:T(2,128)S(1)}, u32[]{:S(2)}, u32[]{:S(2)}) collective-permute-start(f32[2,64,1,96]{3,0,1,2:T(2,128)S(1)} %get-tuple-element.25), channel_id=1, source_target_pairs={{16,0},{32,16},{48,32},{64,48},{80,64},{96,80},{112,96},{128,112},... | collective-permute-start | bytes 147464 | tf_op jit(solution)/shard_map/ppermute | solution.py:20
  242.6 5.7 %collective-permute-done.31 = f32[2,64,1,96]{3,0,1,2:T(2,128)S(1)} collective-permute-done((f32[2,64,1,96]{3,0,1,2:T(2,128)S(1)}, f32[2,64,1,96]{3,0,1,2:T(2,128)S(1)}, u32[]{:S(2)}, u32[]{:S(2)}) %collective-permute-start.31) | collective-permute-done | bytes 49184 | tf_op jit(solution)/shard_map/ppermute | solution.py:20
  248.3 1.3 multiply_add_fusion
  249.8 2.5 fusion.41
  253.2 1.3 multiply_subtract_fusion
  (122 shorter events, 32.4 us)
Async XLA Ops:
  0.6 43.2 %copy-start = (s32[1,9216]{1,0:T(1,128)S(1)}, s32[1,9216]{1,0:T(1,128)}, u32[]{:S(2)}) copy-start(s32[1,9216]{1,0:T(1,128)} %param.14) | copy-start | bytes 110596
  0.6 16.4 %copy-start.3 = (bf16[2,6,1,9216]{3,0,2,1:T(2,128)(2,1)S(1)}, bf16[2,6,1,9216]{3,0,2,1:T(2,128)(2,1)}, u32[]{:S(2)}) copy-start(bf16[2,6,1,9216]{3,0,2,1:T(2,128)(2,1)} %param.9) | copy-start | bytes 663556
  30.2 20.3 %all-to-all-start = ((bf16[32,2,6,1,288]{4,1,2,3,0:T(2,128)(2,1)}), bf16[32,2,6,1,288]{4,1,2,3,0:T(2,128)(2,1)S(1)}, u32[]{:S(2)}, u32[]{:S(2)}) async-start(bf16[32,2,6,1,288]{4,1,2,3,0:T(2,128)(2,1)} %constant_dynamic-update-slice_fusion), calls=%async_computation | async-start | bytes 589824 | tf_op jit(solution)/shard_map/all_to_all | solution.py:98
  41.3 0.7 copy-start.4
  42.3 0.7 copy-start.1
  43.8 0.9 copy-start.2
  44.7 0.8 copy-start.5
  45.5 0.7 copy-start.6
  51.9 24.7 %collective-permute-start = (f32[2,64,1,288]{3,0,1,2:T(2,128)S(1)}, f32[2,64,1,288]{3,0,1,2:T(2,128)S(1)}, u32[]{:S(2)}, u32[]{:S(2)}) collective-permute-start(f32[2,64,1,288]{3,0,1,2:T(2,128)S(1)} %fusion.71), channel_id=1, source_target_pairs={{0,1},{1,2},{2,3},{3,4},{4,5},{5,6},{6,7},{7,8},{8,9},{9,10},{10,1... | collective-permute-start | bytes 442376 | tf_op jit(solution)/shard_map/ppermute | solution.py:20
  53.8 22.8 %collective-permute-start.1 = (f32[2,64,1,288]{3,0,1,2:T(2,128)S(1)}, f32[2,64,1,288]{3,0,1,2:T(2,128)S(1)}, u32[]{:S(2)}, u32[]{:S(2)}) collective-permute-start(f32[2,64,1,288]{3,0,1,2:T(2,128)S(1)} %fusion.71), channel_id=1, source_target_pairs={{1,0},{2,1},{3,2},{4,3},{5,4},{6,5},{7,6},{8,7},{9,8},{10,9},{11,1... | collective-permute-start | bytes 442376 | tf_op jit(solution)/shard_map/ppermute | solution.py:20
  62.2 7.8 %collective-permute-start.2 = (f32[2,64,1,96]{3,0,1,2:T(2,128)S(1)}, f32[2,64,1,96]{3,0,1,2:T(2,128)S(1)}, u32[]{:S(2)}, u32[]{:S(2)}) collective-permute-start(f32[2,64,1,96]{3,0,1,2:T(2,128)S(1)} %get-tuple-element.66), channel_id=1, source_target_pairs={{0,16},{16,32},{32,48},{48,64},{64,80},{80,96},{96,112},{112,128},... | collective-permute-start | bytes 147464 | tf_op jit(solution)/shard_map/ppermute | solution.py:20
  66.5 10.1 %collective-permute-start.3 = (f32[2,64,1,96]{3,0,1,2:T(2,128)S(1)}, f32[2,64,1,96]{3,0,1,2:T(2,128)S(1)}, u32[]{:S(2)}, u32[]{:S(2)}) collective-permute-start(f32[2,64,1,96]{3,0,1,2:T(2,128)S(1)} %get-tuple-element.67), channel_id=1, source_target_pairs={{16,0},{32,16},{48,32},{64,48},{80,64},{96,80},{112,96},{128,112},... | collective-permute-start | bytes 147464 | tf_op jit(solution)/shard_map/ppermute | solution.py:20
  78.2 22.4 %collective-permute-start.4 = (f32[2,64,1,288]{3,0,1,2:T(2,128)S(1)}, f32[2,64,1,288]{3,0,1,2:T(2,128)S(1)}, u32[]{:S(2)}, u32[]{:S(2)}) collective-permute-start(f32[2,64,1,288]{3,0,1,2:T(2,128)S(1)} %broadcast_multiply_fusion), channel_id=1, source_target_pairs={{0,1},{1,2},{2,3},{3,4},{4,5},{5,6},{6,7},{7,8},{8,9},{9,10},{10,1... | collective-permute-start | bytes 442376 | tf_op jit(solution)/shard_map/ppermute | solution.py:20
  80.1 20.5 %collective-permute-start.5 = (f32[2,64,1,288]{3,0,1,2:T(2,128)S(1)}, f32[2,64,1,288]{3,0,1,2:T(2,128)S(1)}, u32[]{:S(2)}, u32[]{:S(2)}) collective-permute-start(f32[2,64,1,288]{3,0,1,2:T(2,128)S(1)} %broadcast_multiply_fusion), channel_id=1, source_target_pairs={{1,0},{2,1},{3,2},{4,3},{5,4},{6,5},{7,6},{8,7},{9,8},{10,9},{11,1... | collective-permute-start | bytes 442376 | tf_op jit(solution)/shard_map/ppermute | solution.py:20
  88.6 6.2 %collective-permute-start.6 = (f32[2,64,1,96]{3,0,1,2:T(2,128)S(1)}, f32[2,64,1,96]{3,0,1,2:T(2,128)S(1)}, u32[]{:S(2)}, u32[]{:S(2)}) collective-permute-start(f32[2,64,1,96]{3,0,1,2:T(2,128)S(1)} %get-tuple-element.60), channel_id=1, source_target_pairs={{0,16},{16,32},{32,48},{48,64},{64,80},{80,96},{96,112},{112,128},... | collective-permute-start | bytes 147464 | tf_op jit(solution)/shard_map/ppermute | solution.py:20
  90.5 10.1 %collective-permute-start.7 = (f32[2,64,1,96]{3,0,1,2:T(2,128)S(1)}, f32[2,64,1,96]{3,0,1,2:T(2,128)S(1)}, u32[]{:S(2)}, u32[]{:S(2)}) collective-permute-start(f32[2,64,1,96]{3,0,1,2:T(2,128)S(1)} %get-tuple-element.61), channel_id=1, source_target_pairs={{16,0},{32,16},{48,32},{64,48},{80,64},{96,80},{112,96},{128,112},... | collective-permute-start | bytes 147464 | tf_op jit(solution)/shard_map/ppermute | solution.py:20
  102.2 22.4 %collective-permute-start.8 = (f32[2,64,1,288]{3,0,1,2:T(2,128)S(1)}, f32[2,64,1,288]{3,0,1,2:T(2,128)S(1)}, u32[]{:S(2)}, u32[]{:S(2)}) collective-permute-start(f32[2,64,1,288]{3,0,1,2:T(2,128)S(1)} %fusion.9), channel_id=1, source_target_pairs={{0,1},{1,2},{2,3},{3,4},{4,5},{5,6},{6,7},{7,8},{8,9},{9,10},{10,1... | collective-permute-start | bytes 442376 | tf_op jit(solution)/shard_map/ppermute | solution.py:20
  104.2 20.5 %collective-permute-start.9 = (f32[2,64,1,288]{3,0,1,2:T(2,128)S(1)}, f32[2,64,1,288]{3,0,1,2:T(2,128)S(1)}, u32[]{:S(2)}, u32[]{:S(2)}) collective-permute-start(f32[2,64,1,288]{3,0,1,2:T(2,128)S(1)} %fusion.9), channel_id=1, source_target_pairs={{1,0},{2,1},{3,2},{4,3},{5,4},{6,5},{7,6},{8,7},{9,8},{10,9},{11,1... | collective-permute-start | bytes 442376 | tf_op jit(solution)/shard_map/ppermute | solution.py:20
  112.6 6.2 %collective-permute-start.10 = (f32[2,64,1,96]{3,0,1,2:T(2,128)S(1)}, f32[2,64,1,96]{3,0,1,2:T(2,128)S(1)}, u32[]{:S(2)}, u32[]{:S(2)}) collective-permute-start(f32[2,64,1,96]{3,0,1,2:T(2,128)S(1)} %get-tuple-element.54), channel_id=1, source_target_pairs={{0,16},{16,32},{32,48},{48,64},{64,80},{80,96},{96,112},{112,128},... | collective-permute-start | bytes 147464 | tf_op jit(solution)/shard_map/ppermute | solution.py:20
  114.5 10.1 %collective-permute-start.11 = (f32[2,64,1,96]{3,0,1,2:T(2,128)S(1)}, f32[2,64,1,96]{3,0,1,2:T(2,128)S(1)}, u32[]{:S(2)}, u32[]{:S(2)}) collective-permute-start(f32[2,64,1,96]{3,0,1,2:T(2,128)S(1)} %get-tuple-element.55), channel_id=1, source_target_pairs={{16,0},{32,16},{48,32},{64,48},{80,64},{96,80},{112,96},{128,112},... | collective-permute-start | bytes 147464 | tf_op jit(solution)/shard_map/ppermute | solution.py:20
  126.6 22.4 %collective-permute-start.12 = (f32[2,64,1,288]{3,0,1,2:T(2,128)S(1)}, f32[2,64,1,288]{3,0,1,2:T(2,128)S(1)}, u32[]{:S(2)}, u32[]{:S(2)}) collective-permute-start(f32[2,64,1,288]{3,0,1,2:T(2,128)S(1)} %fusion.14), channel_id=1, source_target_pairs={{0,1},{1,2},{2,3},{3,4},{4,5},{5,6},{6,7},{7,8},{8,9},{9,10},{10,1... | collective-permute-start | bytes 442376 | tf_op jit(solution)/shard_map/ppermute | solution.py:20
  128.5 20.5 %collective-permute-start.13 = (f32[2,64,1,288]{3,0,1,2:T(2,128)S(1)}, f32[2,64,1,288]{3,0,1,2:T(2,128)S(1)}, u32[]{:S(2)}, u32[]{:S(2)}) collective-permute-start(f32[2,64,1,288]{3,0,1,2:T(2,128)S(1)} %fusion.14), channel_id=1, source_target_pairs={{1,0},{2,1},{3,2},{4,3},{5,4},{6,5},{7,6},{8,7},{9,8},{10,9},{11,1... | collective-permute-start | bytes 442376 | tf_op jit(solution)/shard_map/ppermute | solution.py:20
  137.0 6.2 %collective-permute-start.14 = (f32[2,64,1,96]{3,0,1,2:T(2,128)S(1)}, f32[2,64,1,96]{3,0,1,2:T(2,128)S(1)}, u32[]{:S(2)}, u32[]{:S(2)}) collective-permute-start(f32[2,64,1,96]{3,0,1,2:T(2,128)S(1)} %get-tuple-element.48), channel_id=1, source_target_pairs={{0,16},{16,32},{32,48},{48,64},{64,80},{80,96},{96,112},{112,128},... | collective-permute-start | bytes 147464 | tf_op jit(solution)/shard_map/ppermute | solution.py:20
  138.9 10.1 %collective-permute-start.15 = (f32[2,64,1,96]{3,0,1,2:T(2,128)S(1)}, f32[2,64,1,96]{3,0,1,2:T(2,128)S(1)}, u32[]{:S(2)}, u32[]{:S(2)}) collective-permute-start(f32[2,64,1,96]{3,0,1,2:T(2,128)S(1)} %get-tuple-element.49), channel_id=1, source_target_pairs={{16,0},{32,16},{48,32},{64,48},{80,64},{96,80},{112,96},{128,112},... | collective-permute-start | bytes 147464 | tf_op jit(solution)/shard_map/ppermute | solution.py:20
  151.0 22.4 %collective-permute-start.16 = (f32[2,64,1,288]{3,0,1,2:T(2,128)S(1)}, f32[2,64,1,288]{3,0,1,2:T(2,128)S(1)}, u32[]{:S(2)}, u32[]{:S(2)}) collective-permute-start(f32[2,64,1,288]{3,0,1,2:T(2,128)S(1)} %fusion.19), channel_id=1, source_target_pairs={{0,1},{1,2},{2,3},{3,4},{4,5},{5,6},{6,7},{7,8},{8,9},{9,10},{10,1... | collective-permute-start | bytes 442376 | tf_op jit(solution)/shard_map/ppermute | solution.py:20
  152.9 20.5 %collective-permute-start.17 = (f32[2,64,1,288]{3,0,1,2:T(2,128)S(1)}, f32[2,64,1,288]{3,0,1,2:T(2,128)S(1)}, u32[]{:S(2)}, u32[]{:S(2)}) collective-permute-start(f32[2,64,1,288]{3,0,1,2:T(2,128)S(1)} %fusion.19), channel_id=1, source_target_pairs={{1,0},{2,1},{3,2},{4,3},{5,4},{6,5},{7,6},{8,7},{9,8},{10,9},{11,1... | collective-permute-start | bytes 442376 | tf_op jit(solution)/shard_map/ppermute | solution.py:20
  161.4 6.2 %collective-permute-start.18 = (f32[2,64,1,96]{3,0,1,2:T(2,128)S(1)}, f32[2,64,1,96]{3,0,1,2:T(2,128)S(1)}, u32[]{:S(2)}, u32[]{:S(2)}) collective-permute-start(f32[2,64,1,96]{3,0,1,2:T(2,128)S(1)} %get-tuple-element.42), channel_id=1, source_target_pairs={{0,16},{16,32},{32,48},{48,64},{64,80},{80,96},{96,112},{112,128},... | collective-permute-start | bytes 147464 | tf_op jit(solution)/shard_map/ppermute | solution.py:20
  163.3 10.1 %collective-permute-start.19 = (f32[2,64,1,96]{3,0,1,2:T(2,128)S(1)}, f32[2,64,1,96]{3,0,1,2:T(2,128)S(1)}, u32[]{:S(2)}, u32[]{:S(2)}) collective-permute-start(f32[2,64,1,96]{3,0,1,2:T(2,128)S(1)} %get-tuple-element.43), channel_id=1, source_target_pairs={{16,0},{32,16},{48,32},{64,48},{80,64},{96,80},{112,96},{128,112},... | collective-permute-start | bytes 147464 | tf_op jit(solution)/shard_map/ppermute | solution.py:20
  175.8 22.5 %collective-permute-start.20 = (f32[2,64,1,288]{3,0,1,2:T(2,128)S(1)}, f32[2,64,1,288]{3,0,1,2:T(2,128)S(1)}, u32[]{:S(2)}, u32[]{:S(2)}) collective-permute-start(f32[2,64,1,288]{3,0,1,2:T(2,128)S(1)} %fusion.24), channel_id=1, source_target_pairs={{0,1},{1,2},{2,3},{3,4},{4,5},{5,6},{6,7},{7,8},{8,9},{9,10},{10,1... | collective-permute-start | bytes 442376 | tf_op jit(solution)/shard_map/ppermute | solution.py:20
  177.7 20.6 %collective-permute-start.21 = (f32[2,64,1,288]{3,0,1,2:T(2,128)S(1)}, f32[2,64,1,288]{3,0,1,2:T(2,128)S(1)}, u32[]{:S(2)}, u32[]{:S(2)}) collective-permute-start(f32[2,64,1,288]{3,0,1,2:T(2,128)S(1)} %fusion.24), channel_id=1, source_target_pairs={{1,0},{2,1},{3,2},{4,3},{5,4},{6,5},{7,6},{8,7},{9,8},{10,9},{11,1... | collective-permute-start | bytes 442376 | tf_op jit(solution)/shard_map/ppermute | solution.py:20
  186.2 6.2 %collective-permute-start.22 = (f32[2,64,1,96]{3,0,1,2:T(2,128)S(1)}, f32[2,64,1,96]{3,0,1,2:T(2,128)S(1)}, u32[]{:S(2)}, u32[]{:S(2)}) collective-permute-start(f32[2,64,1,96]{3,0,1,2:T(2,128)S(1)} %get-tuple-element.36), channel_id=1, source_target_pairs={{0,16},{16,32},{32,48},{48,64},{64,80},{80,96},{96,112},{112,128},... | collective-permute-start | bytes 147464 | tf_op jit(solution)/shard_map/ppermute | solution.py:20
  188.1 10.2 %collective-permute-start.23 = (f32[2,64,1,96]{3,0,1,2:T(2,128)S(1)}, f32[2,64,1,96]{3,0,1,2:T(2,128)S(1)}, u32[]{:S(2)}, u32[]{:S(2)}) collective-permute-start(f32[2,64,1,96]{3,0,1,2:T(2,128)S(1)} %get-tuple-element.37), channel_id=1, source_target_pairs={{16,0},{32,16},{48,32},{64,48},{80,64},{96,80},{112,96},{128,112},... | collective-permute-start | bytes 147464 | tf_op jit(solution)/shard_map/ppermute | solution.py:20
  200.7 22.5 %collective-permute-start.24 = (f32[2,64,1,288]{3,0,1,2:T(2,128)S(1)}, f32[2,64,1,288]{3,0,1,2:T(2,128)S(1)}, u32[]{:S(2)}, u32[]{:S(2)}) collective-permute-start(f32[2,64,1,288]{3,0,1,2:T(2,128)S(1)} %fusion.29), channel_id=1, source_target_pairs={{0,1},{1,2},{2,3},{3,4},{4,5},{5,6},{6,7},{7,8},{8,9},{9,10},{10,1... | collective-permute-start | bytes 442376 | tf_op jit(solution)/shard_map/ppermute | solution.py:20
  202.6 20.6 %collective-permute-start.25 = (f32[2,64,1,288]{3,0,1,2:T(2,128)S(1)}, f32[2,64,1,288]{3,0,1,2:T(2,128)S(1)}, u32[]{:S(2)}, u32[]{:S(2)}) collective-permute-start(f32[2,64,1,288]{3,0,1,2:T(2,128)S(1)} %fusion.29), channel_id=1, source_target_pairs={{1,0},{2,1},{3,2},{4,3},{5,4},{6,5},{7,6},{8,7},{9,8},{10,9},{11,1... | collective-permute-start | bytes 442376 | tf_op jit(solution)/shard_map/ppermute | solution.py:20
  211.1 6.2 %collective-permute-start.26 = (f32[2,64,1,96]{3,0,1,2:T(2,128)S(1)}, f32[2,64,1,96]{3,0,1,2:T(2,128)S(1)}, u32[]{:S(2)}, u32[]{:S(2)}) collective-permute-start(f32[2,64,1,96]{3,0,1,2:T(2,128)S(1)} %get-tuple-element.30), channel_id=1, source_target_pairs={{0,16},{16,32},{32,48},{48,64},{64,80},{80,96},{96,112},{112,128},... | collective-permute-start | bytes 147464 | tf_op jit(solution)/shard_map/ppermute | solution.py:20
  213.0 10.2 %collective-permute-start.27 = (f32[2,64,1,96]{3,0,1,2:T(2,128)S(1)}, f32[2,64,1,96]{3,0,1,2:T(2,128)S(1)}, u32[]{:S(2)}, u32[]{:S(2)}) collective-permute-start(f32[2,64,1,96]{3,0,1,2:T(2,128)S(1)} %get-tuple-element.31), channel_id=1, source_target_pairs={{16,0},{32,16},{48,32},{64,48},{80,64},{96,80},{112,96},{128,112},... | collective-permute-start | bytes 147464 | tf_op jit(solution)/shard_map/ppermute | solution.py:20
  225.9 22.4 %collective-permute-start.28 = (f32[2,64,1,288]{3,0,1,2:T(2,128)S(1)}, f32[2,64,1,288]{3,0,1,2:T(2,128)S(1)}, u32[]{:S(2)}, u32[]{:S(2)}) collective-permute-start(f32[2,64,1,288]{3,0,1,2:T(2,128)S(1)} %fusion.34), channel_id=1, source_target_pairs={{0,1},{1,2},{2,3},{3,4},{4,5},{5,6},{6,7},{7,8},{8,9},{9,10},{10,1... | collective-permute-start | bytes 442376 | tf_op jit(solution)/shard_map/ppermute | solution.py:20
  227.8 20.5 %collective-permute-start.29 = (f32[2,64,1,288]{3,0,1,2:T(2,128)S(1)}, f32[2,64,1,288]{3,0,1,2:T(2,128)S(1)}, u32[]{:S(2)}, u32[]{:S(2)}) collective-permute-start(f32[2,64,1,288]{3,0,1,2:T(2,128)S(1)} %fusion.34), channel_id=1, source_target_pairs={{1,0},{2,1},{3,2},{4,3},{5,4},{6,5},{7,6},{8,7},{9,8},{10,9},{11,1... | collective-permute-start | bytes 442376 | tf_op jit(solution)/shard_map/ppermute | solution.py:20
  236.3 6.3 %collective-permute-start.30 = (f32[2,64,1,96]{3,0,1,2:T(2,128)S(1)}, f32[2,64,1,96]{3,0,1,2:T(2,128)S(1)}, u32[]{:S(2)}, u32[]{:S(2)}) collective-permute-start(f32[2,64,1,96]{3,0,1,2:T(2,128)S(1)} %get-tuple-element.24), channel_id=1, source_target_pairs={{0,16},{16,32},{32,48},{48,64},{64,80},{80,96},{96,112},{112,128},... | collective-permute-start | bytes 147464 | tf_op jit(solution)/shard_map/ppermute | solution.py:20
  238.2 10.1 %collective-permute-start.31 = (f32[2,64,1,96]{3,0,1,2:T(2,128)S(1)}, f32[2,64,1,96]{3,0,1,2:T(2,128)S(1)}, u32[]{:S(2)}, u32[]{:S(2)}) collective-permute-start(f32[2,64,1,96]{3,0,1,2:T(2,128)S(1)} %get-tuple-element.25), channel_id=1, source_target_pairs={{16,0},{32,16},{48,32},{64,48},{80,64},{96,80},{112,96},{128,112},... | collective-permute-start | bytes 147464 | tf_op jit(solution)/shard_map/ppermute | solution.py:20
